TPU v7x, 32 devices: a whole 2x2x4 slice. The times are simulated.
32 devices in a mesh: tp: 4 (over z), pp: 8 (over y, x, core).
Axes of the slice: x: 2, y: 2, z: 4, core: 2. Of those that a mesh axis runs over, the one named last changes fastest.
Arguments:
- tokens: bfloat16 [8192, 8192], P('pp', 'tp'), may hold values from -60 to 60
- norm_gain: bfloat16 [8192], P('tp'), may hold values from 0.099609375 to 1.8984375
- weights_gen: bfloat16 [8, 1280, 8192], P('tp', None, 'pp'), may hold values from -2 to 2
- segment_ids: int32 [8, 1024], P('pp'), may hold values from 0 to 15, never falling along the last dimension, each value on 1 to 512 neighbouring positions
Outputs:
- weights_rows: bfloat16 [8, 1280, 8192], P('tp', 'pp')
- attended: bfloat16 [8192, 8192], P('pp', 'tp')
Inputs may be any that keep to these rules, and one draw needn't show every extreme that they name: `segment_ids`: ids never fall along a block; every sequence has 1 to 512 tokens and lies in one block.
All inputs are finite; a program needn't handle non-finite values.
Results may differ from a plain program's by a relative error of at most 0.0075.
Values may be sent and summed in bfloat16 or wider, within the bound.
A program may use at most 192 MiB of HBM per device.

v0:
```python
import functools
import math

import jax
import jax.numpy as jnp
from jax import lax
from jax.experimental import pallas as pl
from jax.experimental.pallas import tpu as pltpu
from jax.sharding import PartitionSpec as P

DH = 128
GROUP = 8
HEADS = GROUP + 2
LANES = 128
MAX_SEQUENCE = 512
ROPE_BASE = 500000.0
EPS = 1e-05
PIECES = 4
MESH = pl.DeviceIdType.MESH
F32 = jnp.float32
BF16 = jnp.bfloat16


def project_kernel(
    n, pn, tokens, gain, seg, weights,
    wall, qkv,
    xr, xn, acc, wbuf, meta, rsb, ctab, stab, stage,
    own_sem, zs_sem, zr_sem, ms_sem, mr_sem, ws_sem, wr_sem, wf_sem, out_sem,
):
    me = lax.axis_index("tp")
    j = lax.axis_index("pp")
    count, local = tokens.shape
    rows, width = weights.shape
    half_rows = rows // 2
    per = local // width
    groups = qkv.shape[0]
    pr = count // PIECES
    rings = pn // 4
    blocks = count // LANES
    core, x, y = j % 2, (j // 2) % 2, j // 4

    def at(y_, x_, core_):
        return (y_ * 2 + x_) * 2 + core_

    j_x = at(y, 1 - x, core)
    j_next = at((y + 1) % rings, x, core)
    j_prev = at((y + rings - 1) % rings, x, core)
    j_pair = at(y, x, 1 - core)

    barrier = pltpu.get_barrier_semaphore()
    for d in range(1, n):
        pl.semaphore_signal(barrier, inc=1, device_id={"tp": (me + d) % n}, device_id_type=MESH)
    for other in (j_x, j_next, j_prev, j_pair):
        pl.semaphore_signal(barrier, inc=1, device_id={"pp": other}, device_id_type=MESH)
    pl.semaphore_wait(barrier, n - 1 + 4)

    def piece(slot, p, up, own=False):
        rng = pl.ds(p * pr, pr)
        return pltpu.make_async_remote_copy(
            src_ref=tokens.at[rng] if own else xr.at[slot, rng],
            dst_ref=xr.at[slot, rng],
            send_sem=zs_sem.at[1 if up else 0, slot, p],
            recv_sem=zr_sem.at[slot, p],
            device_id={"tp": me + 1 if up else me - 1},
            device_id_type=MESH,
        )

    def own_piece(p):
        @pl.when(me < n - 1)
        def _():
            piece(me, p, True, own=True).start()

        @pl.when(me > 0)
        def _():
            piece(me, p, False, own=True).start()

    started = []

    def send_half(link, shard, half, target, own=False):
        rng = pl.ds(half * half_rows, half_rows)
        copy = pltpu.make_async_remote_copy(
            src_ref=weights.at[rng] if own else wall.at[shard, rng],
            dst_ref=wall.at[shard, rng],
            send_sem=ws_sem.at[link, shard, half],
            recv_sem=wr_sem.at[shard, half],
            device_id={"pp": target},
            device_id_type=MESH,
        )
        copy.start()
        started.append(copy)

    def wait_half(shard, half):
        rng = pl.ds(half * half_rows, half_rows)
        pltpu.make_async_copy(wall.at[shard, rng], wall.at[shard, rng], wr_sem.at[shard, half]).wait()

    own_piece(0)
    send_half(0, j, 0, j_x, own=True)
    send_half(1, j, 1, j_next, own=True)
    send_half(0, j, 1, j_x, own=True)
    send_half(1, j, 0, j_next, own=True)
    send_half(2, j, 0, j_pair, own=True)
    send_half(2, j, 1, j_pair, own=True)

    load = pltpu.make_async_copy(tokens, xr.at[me], own_sem)
    load.start()
    load.wait()

    def squares(a, carry):
        v = xr[me, pl.ds(pl.multiple_of(a * LANES, LANES), LANES), :].astype(F32)
        total = jnp.sum(v * v, axis=1, keepdims=True)
        meta[me, pl.ds(a, 1), :] = jnp.broadcast_to(total, (LANES, LANES)).T[0:1, :]
        return carry

    lax.fori_loop(0, blocks, squares, 0)
    meta[me, blocks:, :] = gain[...]

    def meta_copy(d):
        return pltpu.make_async_remote_copy(
            src_ref=meta.at[me],
            dst_ref=meta.at[me],
            send_sem=ms_sem.at[d],
            recv_sem=mr_sem.at[me],
            device_id={"tp": (me + d) % n},
            device_id_type=MESH,
        )

    for d in range(1, n):
        meta_copy(d).start()
    for p in range(1, PIECES):
        own_piece(p)

    lane = lax.broadcasted_iota(jnp.int32, (LANES, LANES), 1)
    freq = jnp.exp((lane % (DH // 2)).astype(F32) * (-2.0 * math.log(ROPE_BASE) / DH))
    sign = jnp.where(lane < DH // 2, -1.0, 1.0)
    ids = seg[...].astype(F32)

    def tables(a, carry):
        rng = pl.ds(pl.multiple_of(a * LANES, LANES), LANES)
        own = jnp.broadcast_to(seg[:, rng].astype(F32), (LANES, LANES)).T[:, 0:1]
        first = jnp.sum(jnp.where(ids < own, 1.0, 0.0), axis=1, keepdims=True)
        order = (lax.broadcasted_iota(jnp.int32, (LANES, LANES), 0) + a * LANES).astype(F32)
        angle = (order - first) * freq
        ctab[rng, :] = jnp.cos(angle)
        stab[rng, :] = jnp.sin(angle) * sign
        return carry

    lax.fori_loop(0, blocks, tables, 0)

    def clear(a, carry):
        rng = pl.ds(pl.multiple_of(a * LANES, LANES), LANES)
        for half in range(2):
            acc[half, rng, :] = jnp.zeros((LANES, half_rows), F32)
        return carry

    lax.fori_loop(0, blocks, clear, 0)

    for d in range(1, n):
        other = (me + d) % n
        pltpu.make_async_copy(meta.at[other], meta.at[other], mr_sem.at[other]).wait()

    def scales(a, carry):
        total = meta[0, pl.ds(a, 1), :]
        for s in range(1, n):
            total = total + meta[s, pl.ds(a, 1), :]
        scale = lax.rsqrt(total * (1.0 / (n * local)) + EPS)
        rsb[pl.ds(pl.multiple_of(a * LANES, LANES), LANES), :] = jnp.broadcast_to(scale, (LANES, LANES)).T
        return carry

    lax.fori_loop(0, blocks, scales, 0)

    def normalise(slot, p):
        def block(a, carry):
            rng = pl.ds(pl.multiple_of(p * pr + a * LANES, LANES), LANES)
            scale = rsb[rng, :]
            for b in range(local // LANES):
                cols = slice(b * LANES, (b + 1) * LANES)
                v = xr[slot, rng, cols].astype(F32) * scale
                xn[slot, rng, cols] = (v * meta[slot, blocks + b : blocks + b + 1, :]).astype(BF16)
            return carry

        lax.fori_loop(0, pr // LANES, block, 0)

    near = jnp.minimum(me, n - 1 - me)

    def slot_of(o):
        pair = jnp.where(o % 2 == 1, me + (o + 1) // 2, me - (o + 1) // 2)
        return jnp.where(o <= 2 * near, pair, jnp.where(me <= n - 1 - me, o, n - 1 - o))

    def arrive(o, p):
        slot = slot_of(o)
        rng = pl.ds(p * pr, pr)
        pltpu.make_async_copy(xr.at[slot, rng], xr.at[slot, rng], zr_sem.at[slot, p]).wait()

        @pl.when((slot > me) & (me > 0))
        def _():
            piece(slot, p, False).start()

        @pl.when((slot < me) & (me < n - 1))
        def _():
            piece(slot, p, True).start()

    def each_piece(p, carry):
        normalise(me, p)
        return carry

    lax.fori_loop(0, PIECES, each_piece, 0)

    def events():
        result = []
        for s in range(1, rings):
            y_s = (y + rings - s) % rings
            on = s < rings - 1
            mine, across = at(y_s, x, core), at(y_s, 1 - x, core)
            result.append([(mine, 1, [(0, j_x)] + ([(1, j_next)] if on else []))])
            if s == 1:
                result[-1].append((j_x, 0, [(1, j_next)]))
            result.append([(mine, 0, [(1, j_next)] if on else [])])
            if s == 1:
                result[-1].append((j_x, 1, []))
            result.append([(across, 0, [(1, j_next)] if on else []), (across, 1, [])])
        return result

    pending = events()

    def take_weights():
        for shard, half, links in pending.pop(0):
            wait_half(shard, half)
            for link, target in links:
                send_half(link, shard, half, target)
            send_half(2, shard, half, j_pair)

    total = (n - 2) * PIECES
    step = max(1, total // len(pending))
    for o in range(1, n - 1):
        for p in range(PIECES):
            arrive(o, p)
            normalise(slot_of(o), p)
            done = (o - 1) * PIECES + p + 1
            if pending and (done + 1) % step == 1 % step and done > 1:
                take_weights()
    while pending:
        take_weights()

    last = n - 1

    @pl.when((me > 0) & (me < n - 1))
    def _():
        for p in range(PIECES):
            arrive(last, p)

    for c in range(pn // 2):
        for half in range(2):
            wait_half(c * 2 + (1 - core), half)

    def fetch(shard, half, buf):
        rng = pl.ds(pl.multiple_of(half * half_rows, half_rows), half_rows)

        @pl.when(shard == j)
        def _():
            pltpu.make_async_copy(weights.at[rng], wbuf.at[buf], wf_sem.at[buf]).start()

        @pl.when(shard != j)
        def _():
            pltpu.make_async_copy(wall.at[shard, rng], wbuf.at[buf], wf_sem.at[buf]).start()

    def fetched(buf):
        pltpu.make_async_copy(weights.at[pl.ds(0, half_rows)], wbuf.at[buf], wf_sem.at[buf]).wait()

    tile = 256 if half_rows % 256 == 0 else 128

    def multiply(slot, q, half, buf, first_row, size):
        rng = pl.ds(first_row, size)
        cols = pl.ds(pl.multiple_of(q * width, width), width)

        def one(t, carry):
            at_ = pl.ds(pl.multiple_of(t * tile, tile), tile)
            acc[half, rng, at_] += lax.dot_general(
                xn[slot, rng, cols], wbuf[buf, at_, :],
                (((1,), (1,)), ((), ())), preferred_element_type=F32,
            )
            return carry

        lax.fori_loop(0, half_rows // tile, one, 0)

    def item_of(it):
        slot = slot_of(it // (per * 2))
        q = (it // 2) % per
        return slot, q, it % 2

    whole = (n - 1) * per * 2

    slot0, q0, half0 = item_of(0)
    fetch(slot0 * per + q0, half0, 0)

    def full(it, carry):
        buf = it % 2
        slot, q, half = item_of(it)
        slot2, q2, half2 = item_of(it + 1)
        fetch(slot2 * per + q2, half2, 1 - buf)
        fetched(buf)
        multiply(slot, q, half, buf, 0, count)
        return carry

    lax.fori_loop(0, whole, full, 0)

    def stage_copy(p):
        return pltpu.make_async_copy(
            stage, qkv.at[:, pl.ds(pl.multiple_of(p * pr, pr), pr), :], out_sem
        )

    heads_half = half_rows // DH
    items = PIECES * per * 2
    slot_last = slot_of(last)

    def tail(it, carry):
        p = it // (per * 2)
        q, half = (it // 2) % per, it % 2
        buf = (whole + it) % 2

        @pl.when(it + 1 < items)
        def _():
            nxt = it + 1
            fetch(slot_last * per + (nxt // 2) % per, nxt % 2, 1 - buf)

        @pl.when(it % (per * 2) == 0)
        def _():
            @pl.when((me == 0) | (me == n - 1))
            def _():
                arrive(last, p)

            normalise(slot_last, p)

        fetched(buf)
        multiply(slot_last, q, half, buf, pl.multiple_of(p * pr, pr), pr)

        @pl.when(it % (per * 2) == per * 2 - 1)
        def _():
            @pl.when(p > 0)
            def _():
                stage_copy(p - 1).wait()

            rng = pl.ds(pl.multiple_of(p * pr, pr), pr)
            cos, sin = ctab[rng, :], stab[rng, :]
            for head in range(groups * HEADS):
                off = head % heads_half * DH
                u = acc[head // heads_half, rng, off : off + DH]
                if head % HEADS < GROUP + 1:
                    u = u * cos + pltpu.roll(u, DH // 2, 1) * sin
                to = head % HEADS * DH
                stage[head // HEADS, :, to : to + DH] = u.astype(BF16)
            stage_copy(p).start()

        return carry

    lax.fori_loop(0, items, tail, 0)
    stage_copy(PIECES - 1).wait()

    for copy in started:
        copy.wait_send()
    for d in range(1, n):
        meta_copy(d).wait_send()

    def drain(i, carry):
        slot, p = i // PIECES, i % PIECES

        @pl.when((slot >= me) & (me > 0))
        def _():
            piece(slot, p, False).wait_send()

        @pl.when((slot <= me) & (me < n - 1))
        def _():
            piece(slot, p, True).wait_send()

        return carry

    lax.fori_loop(0, n * PIECES, drain, 0)


def project(n, pn, groups, tokens, gain, seg, weights):
    count, local = tokens.shape
    rows, width = weights.shape
    half_rows = rows // 2
    metas = (count + local) // LANES
    dma = pltpu.SemaphoreType.DMA
    flops = 2 * count * local * n * rows
    return pl.pallas_call(
        functools.partial(project_kernel, n, pn),
        out_shape=(
            jax.ShapeDtypeStruct((pn, rows, width), BF16),
            jax.ShapeDtypeStruct((groups, count, HEADS * DH), BF16),
        ),
        in_specs=[
            pl.BlockSpec(memory_space=pl.ANY),
            pl.BlockSpec(memory_space=pltpu.VMEM),
            pl.BlockSpec(memory_space=pltpu.VMEM),
            pl.BlockSpec(memory_space=pl.ANY),
        ],
        out_specs=(pl.BlockSpec(memory_space=pl.ANY), pl.BlockSpec(memory_space=pl.ANY)),
        scratch_shapes=[
            pltpu.VMEM((n, count, local), BF16),
            pltpu.VMEM((n, count, local), BF16),
            pltpu.VMEM((2, count, half_rows), F32),
            pltpu.VMEM((2, half_rows, width), BF16),
            pltpu.VMEM((n, metas, LANES), F32),
            pltpu.VMEM((count, LANES), F32),
            pltpu.VMEM((count, LANES), F32),
            pltpu.VMEM((count, LANES), F32),
            pltpu.VMEM((groups, count // PIECES, HEADS * DH), BF16),
            dma,
            dma((2, n, PIECES)),
            dma((n, PIECES)),
            dma((n,)),
            dma((n,)),
            dma((3, pn, 2)),
            dma((pn, 2)),
            dma((2,)),
            dma,
        ],
        compiler_params=pltpu.CompilerParams(
            collective_id=0, has_side_effects=True, vmem_limit_bytes=60 << 20
        ),
        cost_estimate=pl.CostEstimate(flops=flops, bytes_accessed=60 << 20, transcendentals=0),
        name="project",
    )(tokens, gain, seg, weights)


def attend_kernel(
    pn, window, q_ref, k_ref, v_ref, seg, wall, weights, out, rows_out, buf, in_sem, out_sem
):
    g, c = pl.program_id(0), pl.program_id(1)
    steps = pl.num_programs(0) * pl.num_programs(1)
    step = g * pl.num_programs(1) + c
    j = lax.axis_index("pp")
    groups, kept, full = rows_out.shape
    width = full // pn
    row_size = weights.shape[0] // groups

    def pull(gg, s):
        rng = pl.ds(gg * row_size + j * kept, kept)

        @pl.when(s == j)
        def _():
            pltpu.make_async_copy(weights.at[rng], buf.at[gg, s], in_sem.at[gg, s]).start()

        @pl.when(s != j)
        def _():
            pltpu.make_async_copy(wall.at[s, rng], buf.at[gg, s], in_sem.at[gg, s]).start()

    def push(gg, s):
        return pltpu.make_async_copy(
            buf.at[gg, s], rows_out.at[gg, :, pl.ds(s * width, width)], out_sem.at[gg, s]
        )

    @pl.when(step == 0)
    def _():
        for gg in range(groups):
            for s in range(pn):
                pull(gg, s)

    @pl.when(step == 1)
    def _():
        for gg in range(groups):
            for s in range(pn):
                pltpu.make_async_copy(weights.at[pl.ds(0, kept)], buf.at[gg, s], in_sem.at[gg, s]).wait()
                push(gg, s).start()

    back = window - LANES
    base = pl.multiple_of(jnp.maximum(c * LANES - back, 0), LANES)
    rng = pl.ds(base, window)
    own = jnp.broadcast_to(
        seg[:, pl.ds(pl.multiple_of(c * LANES, LANES), LANES)].astype(F32), (LANES, LANES)
    ).T[:, 0:1]
    t = lax.broadcasted_iota(jnp.int32, (LANES, window), 0) + c * LANES
    s = lax.broadcasted_iota(jnp.int32, (LANES, window), 1) + base
    bias = jnp.where((seg[:, rng].astype(F32) == own) & (s <= t), 0.0, -1e30)
    keys = k_ref[0, rng, :]
    values = jnp.concatenate([v_ref[0, rng, :], jnp.ones((window, DH), BF16)], axis=1)
    scale = math.log2(math.e) / math.sqrt(DH)
    for h in range(GROUP):
        cols = slice(h * DH, (h + 1) * DH)
        score = lax.dot_general(
            q_ref[0, :, cols], keys, (((1,), (1,)), ((), ())), preferred_element_type=F32
        )
        score = score * scale + bias
        top = jnp.max(score, axis=1, keepdims=True)
        prob = jnp.exp2(score - top).astype(BF16)
        both = jnp.dot(prob, values, preferred_element_type=F32)
        out[:, cols] = (both[:, :DH] / both[:, DH:]).astype(BF16)

    @pl.when(step == steps - 1)
    def _():
        for gg in range(groups):
            for ss in range(pn):
                push(gg, ss).wait()


def attend(pn, qkv, seg, wall, weights):
    groups, count, _ = qkv.shape
    kept = weights.shape[0] // groups // pn
    width = weights.shape[1]
    window = min(count, MAX_SEQUENCE + LANES)
    dma = pltpu.SemaphoreType.DMA
    return pl.pallas_call(
        functools.partial(attend_kernel, pn, window),
        grid=(groups, count // LANES),
        in_specs=[
            pl.BlockSpec((1, LANES, GROUP * DH), lambda g, c: (g, c, 0)),
            pl.BlockSpec((1, count, DH), lambda g, c: (g, 0, GROUP)),
            pl.BlockSpec((1, count, DH), lambda g, c: (g, 0, GROUP + 1)),
            pl.BlockSpec(memory_space=pltpu.VMEM),
            pl.BlockSpec(memory_space=pl.ANY),
            pl.BlockSpec(memory_space=pl.ANY),
        ],
        out_specs=(
            pl.BlockSpec((LANES, GROUP * DH), lambda g, c: (c, g)),
            pl.BlockSpec(memory_space=pl.ANY),
        ),
        out_shape=(
            jax.ShapeDtypeStruct((count, groups * GROUP * DH), BF16),
            jax.ShapeDtypeStruct((groups, kept, pn * width), BF16),
        ),
        scratch_shapes=[
            pltpu.VMEM((groups, pn, kept, width), BF16),
            dma((groups, pn)),
            dma((groups, pn)),
        ],
        compiler_params=pltpu.CompilerParams(
            dimension_semantics=("arbitrary", "arbitrary"), vmem_limit_bytes=48 << 20
        ),
        name="attend",
    )(qkv, qkv, qkv, seg, wall, weights)


def layer(n, pn, tokens, norm_gain, weights_gen, segment_ids):
    groups, rows, width = weights_gen.shape
    weights = weights_gen.reshape(groups * rows, width)
    gain = norm_gain.astype(F32).reshape(-1, LANES)
    wall, qkv = project(n, pn, groups, tokens, gain, segment_ids, weights)
    attended, weights_rows = attend(pn, qkv, segment_ids, wall, weights)
    return (weights_rows, attended)


def solution(mesh):
    in_specs = (P("pp", "tp"), P("tp"), P("tp", None, "pp"), P("pp", None))
    out_specs = (P("tp", "pp", None), P("pp", "tp"))
    return jax.shard_map(
        functools.partial(layer, mesh.shape["tp"], mesh.shape["pp"]),
        mesh=mesh,
        in_specs=in_specs,
        out_specs=out_specs,
        check_vma=False,
    )
```

profile of v0, /device:TPU:24, one launch (start us, length us, event | category | flops | bytes accessed | tf_op | source)
XLA Modules:
  0.0 349.6 jit_solution(1990317377468760407)
XLA Ops:
  0.6 1.3 bitcast_convert_fusion.gain
  1.9 0.0 copy-start.1
  1.9 318.5 %project.1 = (bf16[8,2560,1024]{2,1,0:T(8,128)(2,1)}, bf16[2,1024,1280]{2,1,0:T(8,128)(2,1)}) custom-call(bf16[1024,2048]{1,0:T(8,128)(2,1)} %tokens.1, f32[16,128]{1,0:T(8,128)} %bitcast_convert_fusion.gain, s32[1,1024]{1,0:T(1,128)} %seg.3, bf16[2560,1024]{1,0:T(8,128)(2,1)} %bitcast.4), custom_call_target="tpu_custom_call" | custom-call | flops 42949672960 | bytes 62914560 | tf_op jit(solution)/shard_map/project/pallas_call | solution.py:386
  320.5 0.0 copy-done.1
  320.5 0.0 copy-start
  320.5 2.5 copy-done
  323.0 26.6 %attend.1 = (bf16[1024,2048]{1,0:T(8,128)(2,1)}, bf16[2,160,8192]{2,1,0:T(8,128)(2,1)}) custom-call(bf16[2,1024,1280]{2,1,0:T(8,128)(2,1)S(1)} %copy-done, bf16[2,1024,1280]{2,1,0:T(8,128)(2,1)S(1)} %copy-done, bf16[2,1024,1280]{2,1,0:T(8,128)(2,1)S(1)} %copy-done, s32[1,1024]{1,0:T(1,128)S(1)} %copy-done.1, bf16[8,2560,1024]{2,1,0:T(8,128)(2,1)} %get-tuple-element.7.wall, ...), custom_call_target="tpu_custom_call" | custom-call | tf_op jit(solution)/shard_map/attend/pallas_call | solution.py:503
Async XLA Ops:
  1.9 318.6 %copy-start.1 = (s32[1,1024]{1,0:T(1,128)S(1)}, s32[1,1024]{1,0:T(1,128)}, u32[]{:S(2)}) copy-start(s32[1,1024]{1,0:T(1,128)} %seg.3) | copy-start | bytes 12292
  320.5 2.5 copy-start
where the time goes:
time: 350 us
  Pallas kernels  345 us (99%)
    pallas_call x1, Pallas kernels, project(): pl.pallas_call(functools.partial(project_kernel, n, pn), out_shape=(jax.S...  319 us
    pallas_call x1, Pallas kernels, attend(): pl.pallas_call(functools.partial(attend_kernel, pn, window), grid=(groups...  26.6 us

commit v1 on v0

v1 whole, which is shorter than its diff:
```python
import functools
import math

import jax
import jax.numpy as jnp
from jax import lax
from jax.experimental import pallas as pl
from jax.experimental.pallas import tpu as pltpu
from jax.sharding import PartitionSpec as P

DH = 128
GROUP = 8
HEADS = GROUP + 2
LANES = 128
MAX_SEQUENCE = 512
ROPE_BASE = 500000.0
EPS = 1e-05
UNITS = 4
MESH = pl.DeviceIdType.MESH
F32 = jnp.float32
BF16 = jnp.bfloat16


def attend_rows(c, base, window, seg, load_q, keys, values, store):
    mine = pl.ds(pl.multiple_of(c * LANES, LANES), LANES)
    own = jnp.broadcast_to(seg[:, mine].astype(F32), (LANES, LANES)).T[:, 0:1]
    t = lax.broadcasted_iota(jnp.int32, (LANES, window), 0) + c * LANES
    s = lax.broadcasted_iota(jnp.int32, (LANES, window), 1) + base
    bias = jnp.where((seg[:, pl.ds(base, window)].astype(F32) == own) & (s <= t), 0.0, -1e30)
    values = jnp.concatenate([values, jnp.ones((window, DH), BF16)], axis=1)
    scale = math.log2(math.e) / math.sqrt(DH)
    for h in range(GROUP):
        cols = slice(h * DH, (h + 1) * DH)
        score = lax.dot_general(
            load_q(cols), keys, (((1,), (1,)), ((), ())), preferred_element_type=F32
        )
        score = score * scale + bias
        top = jnp.max(score, axis=1, keepdims=True)
        prob = jnp.exp2(score - top).astype(BF16)
        both = jnp.dot(prob, values, preferred_element_type=F32)
        store(cols, (both[:, :DH] / both[:, DH:]).astype(BF16))


def project_kernel(
    n, pn, tokens, gain_in, seg_in, weights,
    wall, query, kv_out, att,
    xr, xn, acc, wbuf, meta, rsb, ctab, stab, stage, kv, astage, gain, seg,
    own_sem, zs_sem, zr_sem, ms_sem, mr_sem, ws_sem, wr_sem, wf_sem, out_sem,
):
    me = lax.axis_index("tp")
    j = lax.axis_index("pp")
    count, local = tokens.shape
    rows, width = weights.shape
    half_rows = rows // 2
    per = local // width
    groups = query.shape[0]
    window = min(count, MAX_SEQUENCE + LANES)
    pr = count // UNITS
    big = count // 2
    rings = pn // 4
    blocks = count // LANES
    core, x, y = j % 2, (j // 2) % 2, j // 4

    def at(y_, x_, core_):
        return (y_ * 2 + x_) * 2 + core_

    j_x = at(y, 1 - x, core)
    j_next = at((y + 1) % rings, x, core)
    j_prev = at((y + rings - 1) % rings, x, core)
    j_pair = at(y, x, 1 - core)

    barrier = pltpu.get_barrier_semaphore()
    for d in range(1, n):
        pl.semaphore_signal(barrier, inc=1, device_id={"tp": (me + d) % n}, device_id_type=MESH)
    for other in (j_x, j_next, j_prev, j_pair):
        pl.semaphore_signal(barrier, inc=1, device_id={"pp": other}, device_id_type=MESH)
    pl.semaphore_wait(barrier, n - 1 + 4)

    parts = [(pl.ds(u * pr, pr), slice(None)) for u in range(UNITS - 1)]
    parts += [(pl.ds(count - pr, pr), pl.ds(h * (local // 2), local // 2)) for h in range(2)]

    def piece(slot, p, up, own=False, part=None):
        if part is None:
            index, sem = (pl.ds(pl.multiple_of(p * big, big), big), slice(None)), p
        else:
            index, sem = parts[part], part
        return pltpu.make_async_remote_copy(
            src_ref=tokens.at[index] if own else xr.at[(slot, *index)],
            dst_ref=xr.at[(slot, *index)],
            send_sem=zs_sem.at[1 if up else 0, slot, sem],
            recv_sem=zr_sem.at[slot, sem],
            device_id={"tp": me + 1 if up else me - 1},
            device_id_type=MESH,
        )

    def own_piece(p):
        @pl.when(me < n - 1)
        def _():
            piece(me, p, True, own=True).start()

        @pl.when(me > 0)
        def _():
            piece(me, p, False, own=True).start()

    def pass_on(slot, p, act):
        for up, there, split in (
            (False, (slot > me) & (me > 0), (slot == n - 1) & (me == 1)),
            (True, (slot < me) & (me < n - 1), (slot == 0) & (me == n - 2)),
        ):
            @pl.when(there & jnp.logical_not(split))
            def _():
                act(piece(slot, p, up))

            for half, group in enumerate((range(UNITS // 2), range(UNITS // 2, len(parts)))):
                @pl.when(there & split & (p == half))
                def _():
                    for part in group:
                        act(piece(slot, p, up, part=part))

    started = []

    def send_half(link, shard, half, target, own=False):
        rng = pl.ds(half * half_rows, half_rows)
        copy = pltpu.make_async_remote_copy(
            src_ref=weights.at[rng] if own else wall.at[shard, rng],
            dst_ref=wall.at[shard, rng],
            send_sem=ws_sem.at[link, shard, half],
            recv_sem=wr_sem.at[shard, half],
            device_id={"pp": target},
            device_id_type=MESH,
        )
        copy.start()
        started.append(copy)

    def wait_half(shard, half):
        rng = pl.ds(half * half_rows, half_rows)
        pltpu.make_async_copy(wall.at[shard, rng], wall.at[shard, rng], wr_sem.at[shard, half]).wait()

    own_piece(0)
    send_half(0, j, 0, j_x, own=True)
    send_half(1, j, 1, j_next, own=True)
    send_half(0, j, 1, j_x, own=True)
    send_half(1, j, 0, j_next, own=True)
    send_half(2, j, 0, j_pair, own=True)
    send_half(2, j, 1, j_pair, own=True)

    loads = [
        pltpu.make_async_copy(tokens, xr.at[me], own_sem.at[0]),
        pltpu.make_async_copy(gain_in, gain, own_sem.at[1]),
        pltpu.make_async_copy(seg_in, seg, own_sem.at[2]),
    ]
    for load in loads:
        load.start()
    for load in loads:
        load.wait()

    def squares(a, carry):
        v = xr[me, pl.ds(pl.multiple_of(a * LANES, LANES), LANES), :].astype(F32)
        total = jnp.sum(v * v, axis=1, keepdims=True)
        meta[me, pl.ds(a, 1), :] = jnp.broadcast_to(total, (LANES, LANES)).T[0:1, :]
        return carry

    lax.fori_loop(0, blocks, squares, 0)
    for b in range(local // LANES):
        meta[me, blocks + b : blocks + b + 1, :] = (
            gain[b * LANES : (b + 1) * LANES].astype(F32).reshape(1, LANES)
        )

    def meta_copy(d):
        return pltpu.make_async_remote_copy(
            src_ref=meta.at[me],
            dst_ref=meta.at[me],
            send_sem=ms_sem.at[d],
            recv_sem=mr_sem.at[me],
            device_id={"tp": (me + d) % n},
            device_id_type=MESH,
        )

    for d in range(1, n):
        meta_copy(d).start()
    own_piece(1)

    lane = lax.broadcasted_iota(jnp.int32, (LANES, LANES), 1)
    freq = jnp.exp((lane % (DH // 2)).astype(F32) * (-2.0 * math.log(ROPE_BASE) / DH))
    sign = jnp.where(lane < DH // 2, -1.0, 1.0)
    ids = seg[...].astype(F32)

    def tables(a, carry):
        rng = pl.ds(pl.multiple_of(a * LANES, LANES), LANES)
        own = jnp.broadcast_to(seg[:, rng].astype(F32), (LANES, LANES)).T[:, 0:1]
        first = jnp.sum(jnp.where(ids < own, 1.0, 0.0), axis=1, keepdims=True)
        order = (lax.broadcasted_iota(jnp.int32, (LANES, LANES), 0) + a * LANES).astype(F32)
        angle = (order - first) * freq
        ctab[rng, :] = jnp.cos(angle)
        stab[rng, :] = jnp.sin(angle) * sign
        return carry

    lax.fori_loop(0, blocks, tables, 0)

    def clear(a, carry):
        rng = pl.ds(pl.multiple_of(a * LANES, LANES), LANES)
        for half in range(2):
            acc[half, rng, :] = jnp.zeros((LANES, half_rows), F32)
        for g in range(groups):
            kv[g, rng, :] = jnp.zeros((LANES, 2 * DH), BF16)
        return carry

    lax.fori_loop(0, blocks, clear, 0)

    for d in range(1, n):
        other = (me + d) % n
        pltpu.make_async_copy(meta.at[other], meta.at[other], mr_sem.at[other]).wait()

    def scales(a, carry):
        total = meta[0, pl.ds(a, 1), :]
        for s in range(1, n):
            total = total + meta[s, pl.ds(a, 1), :]
        scale = lax.rsqrt(total * (1.0 / (n * local)) + EPS)
        rsb[pl.ds(pl.multiple_of(a * LANES, LANES), LANES), :] = jnp.broadcast_to(scale, (LANES, LANES)).T
        return carry

    lax.fori_loop(0, blocks, scales, 0)

    def normalise(slot, p, lanes=(0, local // LANES)):
        def block(a, carry):
            rng = pl.ds(pl.multiple_of(p * pr + a * LANES, LANES), LANES)
            scale = rsb[rng, :]
            for b in range(*lanes):
                cols = slice(b * LANES, (b + 1) * LANES)
                v = xr[slot, rng, cols].astype(F32) * scale
                xn[slot, rng, cols] = (v * meta[slot, blocks + b : blocks + b + 1, :]).astype(BF16)
            return carry

        lax.fori_loop(0, pr // LANES, block, 0)

    near = jnp.minimum(me, n - 1 - me)

    def slot_of(o):
        pair = jnp.where(o % 2 == 1, me + (o + 1) // 2, me - (o + 1) // 2)
        return jnp.where(o <= 2 * near, pair, jnp.where(me <= n - 1 - me, o, n - 1 - o))

    def arrive(slot, p):
        rng = pl.ds(pl.multiple_of(p * big, big), big)
        pltpu.make_async_copy(xr.at[slot, rng], xr.at[slot, rng], zr_sem.at[slot, p]).wait()
        pass_on(slot, p, lambda copy: copy.start())

    def each_piece(p, carry):
        normalise(me, p)
        return carry

    lax.fori_loop(0, UNITS, each_piece, 0)

    def events():
        result = []
        for s in range(1, rings):
            y_s = (y + rings - s) % rings
            on = s < rings - 1
            mine, across = at(y_s, x, core), at(y_s, 1 - x, core)
            result.append([(mine, 1, [(0, j_x)] + ([(1, j_next)] if on else []))])
            if s == 1:
                result[-1].append((j_x, 0, [(1, j_next)]))
            result.append([(mine, 0, [(1, j_next)] if on else [])])
            if s == 1:
                result[-1].append((j_x, 1, []))
            result.append([(across, 0, [(1, j_next)] if on else []), (across, 1, [])])
        return result

    pending = events()

    def take_weights():
        for shard, half, links in pending.pop(0):
            wait_half(shard, half)
            for link, target in links:
                send_half(link, shard, half, target)
            send_half(2, shard, half, j_pair)

    def both_ways(u, carry):
        hop, p = u // 2 + 1, u % 2
        above, below = me + hop, me - hop

        @pl.when(above < n)
        def _():
            arrive(above, p)

        @pl.when(below >= 0)
        def _():
            arrive(below, p)

        @pl.when(above < n)
        def _():
            normalise(above, 2 * p)
            normalise(above, 2 * p + 1)

        @pl.when(below >= 0)
        def _():
            normalise(below, 2 * p)
            normalise(below, 2 * p + 1)

        return carry

    def fetch(shard, half, buf):
        rng = pl.ds(pl.multiple_of(half * half_rows, half_rows), half_rows)

        @pl.when(shard == j)
        def _():
            pltpu.make_async_copy(weights.at[rng], wbuf.at[buf], wf_sem.at[buf]).start()

        @pl.when(shard != j)
        def _():
            pltpu.make_async_copy(wall.at[shard, rng], wbuf.at[buf], wf_sem.at[buf]).start()

    def fetched(buf):
        pltpu.make_async_copy(weights.at[pl.ds(0, half_rows)], wbuf.at[buf], wf_sem.at[buf]).wait()

    tile = 256 if half_rows % 256 == 0 else 128

    def multiply(slot, q, half, buf, first_row, size):
        rng = pl.ds(first_row, size)
        cols = pl.ds(pl.multiple_of(q * width, width), width)

        def one(t, carry):
            at_ = pl.ds(pl.multiple_of(t * tile, tile), tile)
            acc[half, rng, at_] += lax.dot_general(
                xn[slot, rng, cols], wbuf[buf, at_, :],
                (((1,), (1,)), ((), ())), preferred_element_type=F32,
            )
            return carry

        lax.fori_loop(0, half_rows // tile, one, 0)

    held = per * 2

    def slot_weights(slot):
        for i in range(held):
            fetch(slot * per + i // 2, i % 2, i)

    def do_slot(slot):
        slot_weights(slot)

        def one(i, carry):
            fetched(i)
            multiply(slot, i // 2, i % 2, i, 0, count)
            return carry

        lax.fori_loop(0, held, one, 0)

    def from_pair(y_, x_):
        for half in range(2):
            wait_half(at(y_, x_, 1 - core), half)

    last = n - 1
    slot_last = slot_of(last)

    stop = (n - 2) * 2
    times = [min(stop, i * half_rows * width // (big * local)) for i in range(1, len(pending) + 1)]
    if n == 4 and rings == 2 and per == 2:
        pairs = [(y, x), (y, 1 - x), (1 - y, x), (1 - y, 1 - x)]
        slots = [y_ * 2 + x_ for y_, x_ in pairs]
        early = [jnp.abs(me - slot) <= 1 for slot in slots[:3]]
        lax.fori_loop(0, 1, both_ways, 0)
        take_weights()
        lax.fori_loop(1, 2, both_ways, 0)
        from_pair(*pairs[0])
        pl.when(early[0])(lambda: do_slot(slots[0]))
        take_weights()
        for r in (1, 2):
            from_pair(*pairs[r])
            pl.when(early[r])(functools.partial(do_slot, slots[r]))
        lax.fori_loop(2, 3, both_ways, 0)
        take_weights()
        lax.fori_loop(3, stop, both_ways, 0)
        from_pair(*pairs[3])
        for r, slot in enumerate(slots):
            late = slot != slot_last
            if r < 3:
                late = late & jnp.logical_not(early[r])
            pl.when(late)(functools.partial(do_slot, slot))
    else:
        now = 0
        for until in times:
            lax.fori_loop(now, until, both_ways, 0)
            now = until
            take_weights()
        lax.fori_loop(now, stop, both_ways, 0)
        for c in range(pn // 2):
            for half in range(2):
                wait_half(c * 2 + (1 - core), half)

        def in_order(o, carry):
            do_slot(slot_of(o))
            return carry

        lax.fori_loop(0, last, in_order, 0)

    slot_weights(slot_last)
    for i in range(held):
        fetched(i)

    heads_half = half_rows // DH
    items = UNITS * held
    subs = pr // LANES

    def kv_copy(p):
        rng = pl.ds(pl.multiple_of(p * pr, pr), pr)
        return pltpu.make_async_copy(kv.at[:, rng, :], kv_out.at[:, rng, :], out_sem.at[0])

    def att_copy(p):
        return pltpu.make_async_copy(
            astage, att.at[:, pl.ds(pl.multiple_of(p * pr, pr), pr), :], out_sem.at[1]
        )

    query_copy = pltpu.make_async_copy(stage, query, out_sem.at[1])

    def rotate(p):
        rng = pl.ds(pl.multiple_of(p * pr, pr), pr)
        cos, sin = ctab[rng, :], stab[rng, :]
        for head in range(groups * HEADS):
            off = head % heads_half * DH
            u = acc[head // heads_half, rng, off : off + DH]
            g, h = head // HEADS, head % HEADS
            if h < GROUP + 1:
                u = u * cos + pltpu.roll(u, DH // 2, 1) * sin
            if h < GROUP:
                stage[g, :, h * DH : (h + 1) * DH] = u.astype(BF16)
            else:
                kv[g, rng, (h - GROUP) * DH : (h - GROUP + 1) * DH] = u.astype(BF16)

    def attention(p):
        def one(i, carry):
            g, sub = i // subs, i % subs
            rows_ = pl.ds(pl.multiple_of(sub * LANES, LANES), LANES)
            c = p * subs + sub
            base = pl.multiple_of(jnp.maximum(c * LANES - (window - LANES), 0), LANES)
            rng = pl.ds(base, window)

            def load_q(cols):
                return stage[g, rows_, cols]

            def store(cols, value):
                astage[g, rows_, cols] = value

            attend_rows(
                c, base, window, seg, load_q, kv[g, rng, :DH], kv[g, rng, DH:], store
            )
            return carry

        lax.fori_loop(0, groups * subs, one, 0)

    def tail(it, carry):
        p, buf = it // held, it % held
        q, half = buf // 2, buf % 2

        end = (me == 0) | (me == n - 1)
        middle = local // LANES // 2

        def take(part):
            view = xr.at[(slot_last, *parts[part])]
            pltpu.make_async_copy(view, view, zr_sem.at[slot_last, part]).wait()

        @pl.when(end & (buf == 0) & (p < UNITS - 1))
        def _():
            for part in range(UNITS - 1):
                pl.when(p == part)(functools.partial(take, part))
            normalise(slot_last, p)

        @pl.when(end & (buf == 0) & (p == UNITS - 1))
        def _():
            take(UNITS - 1)
            normalise(slot_last, UNITS - 1, (0, middle))

        @pl.when(end & (buf == held // 2) & (p == UNITS - 1))
        def _():
            take(UNITS)
            normalise(slot_last, UNITS - 1, (middle, local // LANES))

        multiply(slot_last, q, half, buf, pl.multiple_of(p * pr, pr), pr)

        @pl.when(it % held == held - 1)
        def _():
            rotate(p)

            @pl.when(p > 0)
            def _():
                kv_copy(p - 1).wait()

            kv_copy(p).start()

            @pl.when(p < UNITS - 1)
            def _():
                @pl.when(p > 0)
                def _():
                    att_copy(p - 1).wait()

                attention(p)
                att_copy(p).start()

        return carry

    lax.fori_loop(0, items, tail, 0)
    att_copy(UNITS - 2).wait()
    query_copy.start()
    kv_copy(UNITS - 1).wait()
    query_copy.wait()

    for copy in started:
        copy.wait_send()
    for d in range(1, n):
        meta_copy(d).wait_send()

    def drain(slot, carry):
        for p in range(2):
            @pl.when(slot != me)
            def _():
                pass_on(slot, p, lambda copy: copy.wait_send())

            @pl.when((slot == me) & (me < n - 1))
            def _():
                piece(me, p, True).wait_send()

            @pl.when((slot == me) & (me > 0))
            def _():
                piece(me, p, False).wait_send()

        return carry

    lax.fori_loop(0, n, drain, 0)


def project(n, pn, groups, tokens, gain, seg, weights):
    count, local = tokens.shape
    rows, width = weights.shape
    half_rows = rows // 2
    metas = (count + local) // LANES
    pr = count // UNITS
    held = local // width * 2
    dma = pltpu.SemaphoreType.DMA
    flops = 2 * count * local * n * rows
    return pl.pallas_call(
        functools.partial(project_kernel, n, pn),
        out_shape=(
            jax.ShapeDtypeStruct((pn, rows, width), BF16),
            jax.ShapeDtypeStruct((groups, pr, GROUP * DH), BF16),
            jax.ShapeDtypeStruct((groups, count, 2 * DH), BF16),
            jax.ShapeDtypeStruct((groups, count, GROUP * DH), BF16),
        ),
        in_specs=[pl.BlockSpec(memory_space=pl.ANY)] * 4,
        out_specs=(pl.BlockSpec(memory_space=pl.ANY),) * 4,
        scratch_shapes=[
            pltpu.VMEM((n, count, local), BF16),
            pltpu.VMEM((n, count, local), BF16),
            pltpu.VMEM((2, count, half_rows), F32),
            pltpu.VMEM((held, half_rows, width), BF16),
            pltpu.VMEM((n, metas, LANES), F32),
            pltpu.VMEM((count, LANES), F32),
            pltpu.VMEM((count, LANES), F32),
            pltpu.VMEM((count, LANES), F32),
            pltpu.VMEM((groups, pr, GROUP * DH), BF16),
            pltpu.VMEM((groups, count, 2 * DH), BF16),
            pltpu.VMEM((groups, pr, GROUP * DH), BF16),
            pltpu.VMEM((local,), BF16),
            pltpu.VMEM((1, count), jnp.int32),
            dma((3,)),
            dma((2, n, UNITS + 1)),
            dma((n, UNITS + 1)),
            dma((n,)),
            dma((n,)),
            dma((3, pn, 2)),
            dma((pn, 2)),
            dma((held,)),
            dma((2,)),
        ],
        compiler_params=pltpu.CompilerParams(
            collective_id=0, has_side_effects=True, vmem_limit_bytes=62 << 20
        ),
        cost_estimate=pl.CostEstimate(flops=flops, bytes_accessed=60 << 20, transcendentals=0),
        name="project",
    )(tokens, gain, seg, weights)


def finish_kernel(
    pn, window, q_ref, kv_ref, seg, wall, weights, att, out, rows_out, buf, abuf, obuf, in_sem, out_sem, a_sem, o_sem
):
    g, sub = pl.program_id(0), pl.program_id(1)
    subs = pl.num_programs(1)
    step = g * subs + sub
    j = lax.axis_index("pp")
    groups, kept, full = rows_out.shape
    width = full // pn
    row_size = weights.shape[0] // groups
    count = att.shape[1]
    before = abuf.shape[1]

    def pull(gg, s):
        rng = pl.ds(gg * row_size + j * kept, kept)

        @pl.when(s == j)
        def _():
            pltpu.make_async_copy(weights.at[rng], buf.at[gg, s], in_sem.at[gg, s]).start()

        @pl.when(s != j)
        def _():
            pltpu.make_async_copy(wall.at[s, rng], buf.at[gg, s], in_sem.at[gg, s]).start()

    def push(gg, s):
        return pltpu.make_async_copy(
            buf.at[gg, s], rows_out.at[gg, :, pl.ds(s * width, width)], out_sem.at[gg, s]
        )

    def pull_rows(gg):
        return pltpu.make_async_copy(att.at[gg, pl.ds(0, before)], abuf.at[gg], a_sem.at[0, gg])

    def push_rows(gg):
        return pltpu.make_async_copy(
            abuf.at[gg], out.at[pl.ds(0, before), pl.ds(gg * GROUP * DH, GROUP * DH)], a_sem.at[1, gg]
        )

    @pl.when(step == 0)
    def _():
        for gg in range(groups):
            pull_rows(gg).start()
            for s in range(pn):
                pull(gg, s)

    c = before // LANES + sub
    base = pl.multiple_of(jnp.maximum(c * LANES - (window - LANES), 0), LANES)
    rng = pl.ds(base, window)

    def load_q(cols):
        return q_ref[0, :, cols]

    def store(cols, value):
        obuf[g, sub, :, cols] = value

    attend_rows(c, base, window, seg, load_q, kv_ref[0, rng, :DH], kv_ref[0, rng, DH:], store)

    def put(gg, ss):
        return pltpu.make_async_copy(
            obuf.at[gg, ss],
            out.at[
                pl.ds(pl.multiple_of(before + ss * LANES, LANES), LANES),
                pl.ds(pl.multiple_of(gg * (GROUP * DH), GROUP * DH), GROUP * DH),
            ],
            o_sem.at[gg, ss],
        )

    put(g, sub).start()

    @pl.when(step == 0)
    def _():
        for gg in range(groups):
            pull_rows(gg).wait()
            push_rows(gg).start()
            for s in range(pn):
                pltpu.make_async_copy(weights.at[pl.ds(0, kept)], buf.at[gg, s], in_sem.at[gg, s]).wait()
                push(gg, s).start()

    @pl.when(step == groups * subs - 1)
    def _():
        for gg in range(groups):
            push_rows(gg).wait()
            for s in range(pn):
                push(gg, s).wait()
            for ss in range(obuf.shape[1]):
                put(gg, ss).wait()


def finish(pn, query, kv, att, seg, wall, weights):
    groups, count, _ = kv.shape
    pr = query.shape[1]
    subs = pr // LANES
    kept = weights.shape[0] // groups // pn
    width = weights.shape[1]
    window = min(count, MAX_SEQUENCE + LANES)
    dma = pltpu.SemaphoreType.DMA
    hold = pl.BlockSpec(memory_space=pl.ANY)
    return pl.pallas_call(
        functools.partial(finish_kernel, pn, window),
        grid=(groups, subs),
        in_specs=[
            pl.BlockSpec((1, LANES, GROUP * DH), lambda g, c: (g, c, 0)),
            pl.BlockSpec((1, count, 2 * DH), lambda g, c: (g, 0, 0)),
            pl.BlockSpec(memory_space=pltpu.VMEM),
            hold,
            hold,
            hold,
        ],
        out_specs=(hold, hold),
        out_shape=(
            jax.ShapeDtypeStruct((count, groups * GROUP * DH), BF16),
            jax.ShapeDtypeStruct((groups, kept, pn * width), BF16),
        ),
        scratch_shapes=[
            pltpu.VMEM((groups, pn, kept, width), BF16),
            pltpu.VMEM((groups, count - pr, GROUP * DH), BF16),
            pltpu.VMEM((groups, subs, LANES, GROUP * DH), BF16),
            dma((groups, pn)),
            dma((groups, pn)),
            dma((2, groups)),
            dma((groups, subs)),
        ],
        compiler_params=pltpu.CompilerParams(
            dimension_semantics=("arbitrary", "arbitrary"), vmem_limit_bytes=63 << 20
        ),
        name="finish",
    )(query, kv, seg, wall, weights, att)


def layer(n, pn, tokens, norm_gain, weights_gen, segment_ids):
    groups, rows, width = weights_gen.shape
    weights = weights_gen.reshape(groups * rows, width)
    wall, query, kv, att = project(n, pn, groups, tokens, norm_gain, segment_ids, weights)
    attended, weights_rows = finish(pn, query, kv, att, segment_ids, wall, weights)
    return (weights_rows, attended)


def solution(mesh):
    in_specs = (P("pp", "tp"), P("tp"), P("tp", None, "pp"), P("pp", None))
    out_specs = (P("tp", "pp", None), P("pp", "tp"))
    return jax.shard_map(
        functools.partial(layer, mesh.shape["tp"], mesh.shape["pp"]),
        mesh=mesh,
        in_specs=in_specs,
        out_specs=out_specs,
        check_vma=False,
    )
```

time: 350 us -> 295 us (0.84); the launches traced: 350 us -> 291 us
  Pallas kernels: 345 us -> 290 us
    pallas_call x1, Pallas kernels: 319 us -> 280 us  [project(): pl.pallas_call(functools.partial(project_kernel, n, pn), out_shape=(jax.S...]
    pallas_call x1, Pallas kernels: 26.6 us -> 10.5 us  [finish(): pl.pallas_call(functools.partial(finish_kernel, pn, window), grid=(groups...]
where the time goes in v1:
time: 295 us; the launch traced here: 291 us
  Pallas kernels  290 us (98%)
    pallas_call x1, Pallas kernels, project(): pl.pallas_call(functools.partial(project_kernel, n, pn), out_shape=(jax.S...  280 us
    pallas_call x1, Pallas kernels, finish(): pl.pallas_call(functools.partial(finish_kernel, pn, window), grid=(groups...  10.5 us

profile of v1, /device:TPU:24, one launch (start us, length us, event | category | flops | bytes accessed | tf_op | source)
XLA Modules:
  0.0 291.0 jit_solution(6734705897637733670)
XLA Ops:
  0.6 279.9 %project.1 = (bf16[8,2560,1024]{2,1,0:T(8,128)(2,1)}, bf16[2,256,1024]{2,1,0:T(8,128)(2,1)}, bf16[2,1024,256]{2,1,0:T(8,128)(2,1)}, bf16[2,1024,1024]{2,1,0:T(8,128)(2,1)}) custom-call(bf16[1024,2048]{1,0:T(8,128)(2,1)} %tokens.1, bf16[2048]{0:T(1024)(128)(2,1)} %gain_in.1, s32[1,1024]{1,0:T(1,128)} %seg.1, bf16[2560,1024]{1,0:T(8,128)(2,1)} %bitcast.1), custom_call_target="tpu_custom_call" | custom-call | flops 42949672960 | bytes 62914560 | tf_op jit(solution)/shard_map/project/pallas_call | solution.py:538
  280.6 10.5 %finish.1 = (bf16[1024,2048]{1,0:T(8,128)(2,1)}, bf16[2,160,8192]{2,1,0:T(8,128)(2,1)}) custom-call(bf16[2,256,1024]{2,1,0:T(8,128)(2,1)} %get-tuple-element.8.q_ref, bf16[2,1024,256]{2,1,0:T(8,128)(2,1)} %get-tuple-element.9.kv_ref, s32[1,1024]{1,0:T(1,128)} %seg.1, bf16[8,2560,1024]{2,1,0:T(8,128)(2,1)} %get-tuple-element.10.wall, ...), custom_call_target="tpu_custom_call" | custom-call | tf_op jit(solution)/shard_map/finish/pallas_call | solution.py:676

commit v2 on v1

--- a/solution.py
+++ b/solution.py
@@ -327,6 +327,18 @@
             return carry
 
         lax.fori_loop(0, half_rows // tile, one, 0)
+
+    chunk = 640 if half_rows % 640 == 0 else half_rows
+
+    def multiply_few(slot, q, half, buf, first_row, size):
+        rng = pl.ds(first_row, size)
+        cols = pl.ds(pl.multiple_of(q * width, width), width)
+        for t in range(half_rows // chunk):
+            out = lax.dot_general(
+                wbuf[buf, t * chunk : (t + 1) * chunk, :], xn[slot, rng, cols],
+                (((1,), (1,)), ((), ())), preferred_element_type=F32,
+            )
+            acc[half, rng, t * chunk : (t + 1) * chunk] += out.T
 
     held = per * 2
 
@@ -473,7 +485,7 @@
             take(UNITS)
             normalise(slot_last, UNITS - 1, (middle, local // LANES))
 
-        multiply(slot_last, q, half, buf, pl.multiple_of(p * pr, pr), pr)
+        multiply_few(slot_last, q, half, buf, pl.multiple_of(p * pr, pr), pr)
 
         @pl.when(it % held == held - 1)
         def _():

time: 295 us -> 294 us (level)
  no operation moved by 1% of the time
where the time goes in v2:
time: 294 us; the launch traced here: 290 us
  Pallas kernels  289 us (98%)
    pallas_call x1, Pallas kernels, project(): pl.pallas_call(functools.partial(project_kernel, n, pn), out_shape=(jax.S...  279 us
    pallas_call x1, Pallas kernels, finish(): pl.pallas_call(functools.partial(finish_kernel, pn, window), grid=(groups...  10.5 us

profile of v2, /device:TPU:24, one launch (start us, length us, event | category | flops | bytes accessed | tf_op | source)
XLA Modules:
  0.0 290.1 jit_solution(17608511639052728428)
XLA Ops:
  0.6 278.8 %project.1 = (bf16[8,2560,1024]{2,1,0:T(8,128)(2,1)}, bf16[2,256,1024]{2,1,0:T(8,128)(2,1)}, bf16[2,1024,256]{2,1,0:T(8,128)(2,1)}, bf16[2,1024,1024]{2,1,0:T(8,128)(2,1)}) custom-call(bf16[1024,2048]{1,0:T(8,128)(2,1)} %tokens.1, bf16[2048]{0:T(1024)(128)(2,1)} %gain_in.1, s32[1,1024]{1,0:T(1,128)} %seg.1, bf16[2560,1024]{1,0:T(8,128)(2,1)} %bitcast.1), custom_call_target="tpu_custom_call" | custom-call | flops 42949672960 | bytes 62914560 | tf_op jit(solution)/shard_map/project/pallas_call | solution.py:550
  279.4 10.5 %finish.1 = (bf16[1024,2048]{1,0:T(8,128)(2,1)}, bf16[2,160,8192]{2,1,0:T(8,128)(2,1)}) custom-call(bf16[2,256,1024]{2,1,0:T(8,128)(2,1)} %get-tuple-element.8.q_ref, bf16[2,1024,256]{2,1,0:T(8,128)(2,1)} %get-tuple-element.9.kv_ref, s32[1,1024]{1,0:T(1,128)} %seg.1, bf16[8,2560,1024]{2,1,0:T(8,128)(2,1)} %get-tuple-element.10.wall, ...), custom_call_target="tpu_custom_call" | custom-call | tf_op jit(solution)/shard_map/finish/pallas_call | solution.py:688
